TPU v7x, 512 devices: a whole 4x8x8 slice. The times are simulated.
512 devices in a mesh: kgrp: 128 (over y, x, z_hi), img: 4 (over z_lo, core).
Axes of the slice: x: 4, y: 8, z: 8 (z_hi: 4, z_lo: 2; z = z_hi * 2 + z_lo), core: 2. Of those that a mesh axis runs over, the one named last changes fastest.
Arguments:
- vectors: float32 [2, 16, 16384], P(None, 'img', 'kgrp'), may hold values from -6 to 6
- conduction: bfloat16 [256, 2, 8, 4, 4096], P('kgrp', None, None, 'img'), may hold values from -6 to 6
- valence: bfloat16 [256, 2, 8, 4, 4096], P('kgrp', None, None, 'img'), may hold values from -6 to 6
- hole_point: int32 [1], replicated, may hold values from 0 to 16383
- kpoint_grid: int32 [3, 256], replicated, may hold values from 0 to 11
- image_cells: int32 [3, 512], replicated, may hold values from -6 to 6
Outputs:
- psi_real: float32 [16, 4, 4096, 512], P(None, 'img', 'kgrp')
- psi_imag: float32 [16, 4, 4096, 512], P(None, 'img', 'kgrp')
All inputs are finite; a program needn't handle non-finite values.
Results may differ from a plain program's by a relative error of at most 0.0043.
Values may be sent and summed in bfloat16 or wider, within the bound.
A program may use at most 64 MiB of HBM per device.

v0:
```python
import jax
import jax.numpy as jnp
import numpy as np
from jax import lax
from jax.sharding import PartitionSpec as P

NV = 8
NC = 8
cosine_levels = np.cos(2.0 * np.pi * np.arange(12) / 12.0)
sine_levels = np.sin(2.0 * np.pi * np.arange(12) / 12.0)


def phase_table(kpoint_grid, image_cells):
    turn_count = kpoint_grid[0][:, None] * image_cells[0][None, :]
    turn_count = turn_count + kpoint_grid[1][:, None] * image_cells[1][None, :]
    turn_count = turn_count + kpoint_grid[2][:, None] * image_cells[2][None, :]
    turn_count = jnp.mod(turn_count, 12)
    cosine = jnp.zeros(turn_count.shape, jnp.float32)
    sine_part = jnp.zeros(turn_count.shape, jnp.float32)
    for level_index in range(12):
        matches = turn_count == level_index
        cosine = jnp.where(matches, jnp.float32(cosine_levels[level_index]), cosine)
        sine_part = jnp.where(matches, jnp.float32(sine_levels[level_index]), sine_part)
    upper_half = jnp.stack([cosine, sine_part], 1)
    lower_half = jnp.stack([-sine_part, cosine], 1)
    return jnp.stack([upper_half, lower_half], 0).astype(jnp.bfloat16)


def hole_weights(amplitudes, hole_values):
    norm_factor = (NV * NC) ** (-0.5)
    real_amplitude = amplitudes[0]
    imaginary_amplitude = amplitudes[1]
    real_hole = hole_values[:, 0]
    imaginary_hole = hole_values[:, 1]
    highest = lax.Precision.HIGHEST
    weight_real = jnp.einsum("skvc,kv->ksc", real_amplitude, real_hole, precision=highest)
    weight_real = weight_real + jnp.einsum(
        "skvc,kv->ksc", imaginary_amplitude, imaginary_hole, precision=highest
    )
    weight_imaginary = jnp.einsum("skvc,kv->ksc", imaginary_amplitude, real_hole, precision=highest)
    weight_imaginary = weight_imaginary - jnp.einsum(
        "skvc,kv->ksc", real_amplitude, imaginary_hole, precision=highest
    )
    return jnp.stack([weight_real * norm_factor, weight_imaginary * norm_factor], 1).astype(
        jnp.bfloat16
    )


def mixing(weights):
    weight_real = weights[:, 0]
    weight_imaginary = weights[:, 1]
    first_row = jnp.stack([weight_real, -weight_imaginary], 2)
    second_row = jnp.stack([weight_imaginary, weight_real], 2)
    return jnp.stack([first_row, second_row], 1)


def shards(vectors, conduction, valence, hole_point, kpoint_grid, image_cells):
    group_size = lax.axis_size("kgrp")
    local_k = conduction.shape[0]
    slab_width = conduction.shape[4]
    own_excitons = vectors.shape[1]
    blocks = vectors.shape[2] // group_size
    columns = vectors.reshape(2, own_excitons, group_size, blocks)
    owned_columns = lax.all_to_all(columns, "kgrp", split_axis=2, concat_axis=2, tiled=True)
    owned_columns = owned_columns.reshape(2, own_excitons, local_k, NV, NC)
    hole_offset = hole_point[0] % slab_width
    hole_slab = hole_point[0] // slab_width
    present = (lax.axis_index("img") == hole_slab).astype(jnp.float32)
    picked = (
        lax.dynamic_slice_in_dim(valence[:, :, :, 0, :], hole_offset, 1, 3)[..., 0].astype(
            jnp.float32
        )
        * present
    )
    hole_values = lax.psum(picked, "img")
    all_columns = lax.all_gather(owned_columns, "img", axis=1, tiled=True)
    weights = hole_weights(all_columns, hole_values)
    phases = phase_table(kpoint_grid, image_cells)
    products = jnp.einsum(
        "kasbc,kbcp->sakp",
        mixing(weights),
        conduction[:, :, :, 0, :],
        preferred_element_type=jnp.float32,
    ).astype(jnp.bfloat16)
    summed = jnp.einsum(
        "sakp,akbn->spbn",
        lax.all_to_all(products, "kgrp", split_axis=3, concat_axis=2, tiled=True),
        phases,
        preferred_element_type=jnp.float32,
    )
    normal_scale = (2 * kpoint_grid.shape[1]) ** (-0.5)
    summed = summed * normal_scale
    return (summed[:, None, :, 0, :], summed[:, None, :, 1, :])


def solution(mesh):
    placed = (
        P(None, "img", "kgrp"),
        P("kgrp", None, None, "img", None),
        P("kgrp", None, None, "img", None),
        P(),
        P(),
        P(),
    )
    return jax.shard_map(
        shards,
        mesh=mesh,
        in_specs=placed,
        out_specs=(P(None, "img", "kgrp", None), P(None, "img", "kgrp", None)),
        check_vma=False,
    )
```

profile of v0, /device:TPU:8, one launch (start us, length us, event | category | flops | bytes accessed | tf_op | source)
XLA Modules:
  0.0 111.9 jit_solution(5236022632202495821)
XLA Ops:
  0.6 0.0 copy-start
  0.6 1.5 %copy.29 = f32[2,4,128]{1,0,2:T(2,128)} copy(f32[2,4,128]{2,1,0:T(4,128)} %param.6) | data formatting | bytes 8192 | tf_op args[0]
  2.2 19.8 %all-to-all-start = ((f32[2,4,128,1]{1,0,3,2:T(2,128)}), f32[2,4,128,1]{1,0,3,2:T(2,128)S(1)}, u32[]{:S(2)}, u32[]{:S(2)}) async-start(f32[2,4,128,1]{1,0,3,2:T(2,128)} %bitcast.4), calls=%async_computation | async-start | bytes 262144 | tf_op jit(solution)/shard_map/all_to_all | solution.py:64
  22.7 0.9 multiply_reduce_fusion
  23.5 6.3 %psum.7 = f32[2,2,8]{2,1,0:T(2,128)S(1)} all-reduce(f32[2,2,8]{2,1,0:T(2,128)S(1)} %multiply_reduce_fusion), channel_id=1, replica_groups=mesh['kgrp'=128,'img'=4] {'img'}, use_global_device_ids=true, to_apply=%region_0.1 | all-reduce | flops 32 | bytes 256 | tf_op jit(solution)/shard_map/psum | solution.py:75
  29.9 6.6 %all-to-all-done = f32[2,4,128,1]{1,0,3,2:T(2,128)S(1)} async-done(((f32[2,4,128,1]{1,0,3,2:T(2,128)}), f32[2,4,128,1]{1,0,3,2:T(2,128)S(1)}, u32[]{:S(2)}, u32[]{:S(2)}) %all-to-all-start) | async-done | bytes 4128 | tf_op jit(solution)/shard_map/all_to_all | solution.py:64
  36.5 0.3 copy.30
  36.8 5.8 %all_gather.3 = f32[2,16,2,8,8]{4,3,2,0,1:T(8,128)S(1)} all-gather(f32[2,4,2,8,8]{4,3,2,0,1:T(8,128)S(1)} %copy.30), channel_id=1, replica_groups=mesh['kgrp'=128,'img'=4] {'img'}, dimensions={1}, use_global_device_ids=true | all-gather | bytes 20480 | tf_op jit(solution)/shard_map/all_gather | solution.py:76
  42.6 0.3 fusion.15
  42.8 0.3 fusion.13
  43.1 0.3 fusion.19
  43.4 0.3 fusion.17
  43.6 0.1 copy.41
  43.7 0.1 copy.44
  43.8 0.1 copy.45
  43.8 0.1 copy.46
  43.9 0.0 copy-done
  43.9 0.3 fusion.1
  44.3 7.1 %copy.32 = bf16[16,2,2,4096]{0,1,2,3:T(2,128)(2,1)} copy(bf16[16,2,2,4096]{3,0,1,2:T(8,128)(2,1)S(1)} %fusion.1) | data formatting | bytes 1048576 | tf_op jit(solution)/shard_map/convert_element_type | solution.py:84
  51.4 0.0 copy-start.2
  51.4 0.0 copy-start.1
  51.4 12.9 %reshape.653 = bf16[128,2,1024]{2,1,0:T(2,128)(2,1)} reshape(bf16[4096,2,2,16]{3,2,1,0:T(2,128)(2,1)} %bitcast.114) | data formatting | bytes 1048576
  64.3 9.2 %all-to-all-start.1 = ((bf16[128,2,1024]{2,1,0:T(2,128)(2,1)}), bf16[128,2,1024]{2,1,0:T(2,128)(2,1)S(1)}, u32[]{:S(2)}, u32[]{:S(2)}) async-start(bf16[128,2,1024]{2,1,0:T(2,128)(2,1)} %reshape.653), calls=%async_computation.1 | async-start | bytes 1048576 | tf_op jit(solution)/shard_map/all_to_all | solution.py:87
  73.5 0.0 copy-done.2
  73.6 0.0 copy-done.1
  73.6 1.1 fusion.12
  74.6 0.1 maximum_bitcast_fusion.2
  74.7 22.0 %all-to-all-done.1 = bf16[128,2,1024]{2,1,0:T(2,128)(2,1)S(1)} async-done(((bf16[128,2,1024]{2,1,0:T(2,128)(2,1)}), bf16[128,2,1024]{2,1,0:T(2,128)(2,1)S(1)}, u32[]{:S(2)}, u32[]{:S(2)}) %all-to-all-start.1) | async-done | bytes 524320 | tf_op jit(solution)/shard_map/all_to_all | solution.py:87
  96.8 4.1 %reshape.654 = bf16[4096,2,2,16]{3,2,1,0:T(2,128)(2,1)} reshape(bf16[128,2,1024]{2,1,0:T(2,128)(2,1)S(1)} %all-to-all-done.1) | data formatting | bytes 1048576
  100.9 8.6 %copy.52 = bf16[16,2,2,128,32]{4,0,2,3,1:T(8,128)(2,1)S(1)} copy(bf16[16,2,2,128,32]{0,1,2,4,3:T(2,128)(2,1)} %bitcast.115) | data formatting | bytes 1048576 | tf_op jit(solution)/shard_map/all_to_all | solution.py:87
  109.5 1.0 bitcast_multiply_fusion
  110.4 1.5 %slice_bitcast_fusion = (f32[16,1,32,512]{3,2,1,0:T(8,128)}, f32[16,1,32,512]{3,2,1,0:T(8,128)}) fusion(f32[16,32,2,512]{3,1,2,0:T(8,128)S(1)} %bitcast_multiply_fusion), kind=kLoop, calls=%fused_computation.6 | loop fusion | bytes 4194304
  (6 shorter events, 0.1 us)
Async XLA Ops:
  0.6 43.3 %copy-start = (bf16[2,2,8,1,4096]{4,2,3,1,0:T(8,128)(2,1)S(1)}, bf16[2,2,8,1,4096]{4,2,3,1,0:T(8,128)(2,1)}, u32[]{:S(2)}) copy-start(bf16[2,2,8,1,4096]{4,2,3,1,0:T(8,128)(2,1)} %param.7) | copy-start | bytes 786436
  2.2 34.3 %all-to-all-start = ((f32[2,4,128,1]{1,0,3,2:T(2,128)}), f32[2,4,128,1]{1,0,3,2:T(2,128)S(1)}, u32[]{:S(2)}, u32[]{:S(2)}) async-start(f32[2,4,128,1]{1,0,3,2:T(2,128)} %bitcast.4), calls=%async_computation | async-start | bytes 262144 | tf_op jit(solution)/shard_map/all_to_all | solution.py:64
  51.4 22.1 %copy-start.2 = (s32[3,256]{1,0:T(4,128)S(1)}, s32[3,256]{1,0:T(4,128)}, u32[]{:S(2)}) copy-start(s32[3,256]{1,0:T(4,128)} %param.10) | copy-start | bytes 9220
  51.4 22.1 %copy-start.1 = (s32[3,512]{1,0:T(4,128)S(1)}, s32[3,512]{1,0:T(4,128)}, u32[]{:S(2)}) copy-start(s32[3,512]{1,0:T(4,128)} %param.11) | copy-start | bytes 18436
  64.3 32.4 %all-to-all-start.1 = ((bf16[128,2,1024]{2,1,0:T(2,128)(2,1)}), bf16[128,2,1024]{2,1,0:T(2,128)(2,1)S(1)}, u32[]{:S(2)}, u32[]{:S(2)}) async-start(bf16[128,2,1024]{2,1,0:T(2,128)(2,1)} %reshape.653), calls=%async_computation.1 | async-start | bytes 1048576 | tf_op jit(solution)/shard_map/all_to_all | solution.py:87
where the time goes:
time: 112 us
  local copies, waits for them, and re-layouts  36.4 us (32%)
  starting transfers between devices  29 us (26%)
  waiting for transfers between devices  28.6 us (26%)
  blocking collectives  12.1 us (11%)
  matrix products  2.31 us (2%)
  other arithmetic  2.02 us (2%)
  between operations  1.47 us (1%)
    all_to_all x1, waiting for transfers between devices, shards(): lax.all_to_all(products, 'kgrp', split_axis=3, concat_axis=2, tiled=True)  22 us
    unnamed x10, local copies, waits for them, and re-layouts  20.1 us
    all_to_all x1, starting transfers between devices, shards(): lax.all_to_all(columns, 'kgrp', split_axis=2, concat_axis=2, tiled=True)  19.8 us
    all_to_all x1, starting transfers between devices, shards(): lax.all_to_all(products, 'kgrp', split_axis=3, concat_axis=2, tiled=True)  9.2 us
    all_to_all x1, local copies, waits for them, and re-layouts, shards(): lax.all_to_all(products, 'kgrp', split_axis=3, concat_axis=2, tiled=True)  8.56 us
    convert_element_type x1, local copies, waits for them, and re-layouts, shards(): products = jnp.einsum('kasbc,kbcp->sakp', mixing(weights), conduction[:,...  7.13 us
    all_to_all x1, waiting for transfers between devices, shards(): lax.all_to_all(columns, 'kgrp', split_axis=2, concat_axis=2, tiled=True)  6.61 us
    psum x1, blocking collectives, shards(): hole_values = lax.psum(picked, 'img')  6.33 us
  transfers between devices with their start and end apart: 2, of which 2 were waited for; matrix products, arithmetic and copies ran while one was open for 2% of the time, Pallas kernels for 0%

commit v1 on v0

--- a/solution.py
+++ b/solution.py
@@ -73,7 +73,9 @@
         * present
     )
     hole_values = lax.psum(picked, "img")
-    all_columns = lax.all_gather(owned_columns, "img", axis=1, tiled=True)
+    all_columns = jnp.concatenate(
+        lax.all_to_all(jnp.stack([owned_columns] * lax.axis_size("img")), "img", 0, 0), axis=1
+    )
     weights = hole_weights(all_columns, hole_values)
     phases = phase_table(kpoint_grid, image_cells)
     products = jnp.einsum(

time: 112 us -> 116 us (1.036)
  the two profiles are of different devices: /device:TPU:8 before, /device:TPU:64 now
where the time goes in v1:
time: 116 us; the launch traced here: 115 us
  blocking collectives  39.7 us (34%)
  local copies, waits for them, and re-layouts  37.2 us (32%)
  waiting for transfers between devices  21.9 us (19%)
  starting transfers between devices  10.1 us (9%)
  other arithmetic  2.71 us (2%)
  matrix products  2.3 us (2%)
  between operations  1.5 us (1%)
    all_to_all x1, blocking collectives, shards(): lax.all_to_all(columns, 'kgrp', split_axis=2, concat_axis=2, tiled=True)  34 us
    all_to_all x1, waiting for transfers between devices, shards(): lax.all_to_all(products, 'kgrp', split_axis=3, concat_axis=2, tiled=True)  21.9 us
    unnamed x12, local copies, waits for them, and re-layouts  20.4 us
    all_to_all x1, local copies, waits for them, and re-layouts, shards(): lax.all_to_all(products, 'kgrp', split_axis=3, concat_axis=2, tiled=True)  8.56 us
    convert_element_type x1, local copies, waits for them, and re-layouts, shards(): products = jnp.einsum('kasbc,kbcp->sakp', mixing(weights), conduction[:,...  7.14 us
    all_to_all x1, starting transfers between devices, shards(): lax.all_to_all(products, 'kgrp', split_axis=3, concat_axis=2, tiled=True)  6.36 us
    psum x1, blocking collectives, shards(): hole_values = lax.psum(picked, 'img')  5.75 us
    all_to_all x1, starting transfers between devices, shards(): lax.all_to_all(jnp.stack([owned_columns] * lax.axis_size('img')), 'img',...  3.78 us
  transfers between devices with their start and end apart: 2, of which 1 were waited for; matrix products, arithmetic and copies ran while one was open for 2% of the time, Pallas kernels for 0%

profile of v1, /device:TPU:64, one launch (start us, length us, event | category | flops | bytes accessed | tf_op | source)
XLA Modules:
  0.0 115.5 jit_solution(3595970362202070796)
XLA Ops:
  0.6 0.0 copy-start
  0.6 0.9 copy.20
  1.5 34.0 %all_to_all.28 = f32[2,4,128,1]{1,0,3,2:T(2,128)S(1)} all-to-all(f32[2,4,128,1]{1,0,3,2:T(2,128)S(1)} %bitcast.122), channel_id=1, replica_groups=mesh['kgrp'=128,'img'=4] {'kgrp'}, dimensions={2} | all-to-all | bytes 8192 | tf_op jit(solution)/shard_map/all_to_all | solution.py:64
  35.5 0.3 copy.21
  35.8 0.8 reshape.660
  36.6 3.8 %all-to-all-start.1 = ((f32[4,1,1024]{2,1,0:T(1,128)}), f32[4,1,1024]{2,1,0:T(1,128)S(1)}, u32[]{:S(2)}, u32[]{:S(2)}) async-start(f32[4,1,1024]{2,1,0:T(1,128)} %reshape.660), calls=%async_computation.1 | async-start | bytes 32768 | tf_op jit(solution)/shard_map/all_to_all | solution.py:77
  41.0 0.9 multiply_reduce_fusion
  41.9 5.8 %psum.7 = f32[2,2,8]{2,1,0:T(2,128)S(1)} all-reduce(f32[2,2,8]{2,1,0:T(2,128)S(1)} %multiply_reduce_fusion), channel_id=1, replica_groups=mesh['kgrp'=128,'img'=4] {'img'}, use_global_device_ids=true, to_apply=%region_0.1 | all-reduce | flops 32 | bytes 256 | tf_op jit(solution)/shard_map/psum | solution.py:75
  47.6 0.0 all-to-all-done.1
  47.6 0.5 broadcast.741
  48.2 0.7 reduce.2
  48.9 0.2 reshape.661
  49.1 0.3 fusion.15
  49.3 0.3 fusion.13
  49.6 0.3 fusion.19
  49.8 0.3 fusion.17
  50.1 0.1 copy.32
  50.2 0.1 copy.35
  50.2 0.1 copy.36
  50.3 0.1 copy.37
  50.4 0.0 copy-done
  50.4 0.3 fusion.1
  50.8 7.1 %copy.23 = bf16[16,2,2,4096]{0,1,2,3:T(2,128)(2,1)} copy(bf16[16,2,2,4096]{3,0,1,2:T(8,128)(2,1)S(1)} %fusion.1) | data formatting | bytes 1048576 | tf_op jit(solution)/shard_map/convert_element_type | solution.py:86
  57.9 0.0 copy-start.2
  57.9 0.0 copy-start.1
  57.9 12.9 %reshape.662 = bf16[128,2,1024]{2,1,0:T(2,128)(2,1)} reshape(bf16[4096,2,2,16]{3,2,1,0:T(2,128)(2,1)} %bitcast.113) | data formatting | bytes 1048576
  70.8 6.4 %all-to-all-start.2 = ((bf16[128,2,1024]{2,1,0:T(2,128)(2,1)}), bf16[128,2,1024]{2,1,0:T(2,128)(2,1)S(1)}, u32[]{:S(2)}, u32[]{:S(2)}) async-start(bf16[128,2,1024]{2,1,0:T(2,128)(2,1)} %reshape.662), calls=%async_computation.2 | async-start | bytes 1048576 | tf_op jit(solution)/shard_map/all_to_all | solution.py:89
  77.2 0.0 copy-done.2
  77.2 0.0 copy-done.1
  77.2 1.1 fusion.12
  78.3 0.1 maximum_bitcast_fusion.2
  78.4 21.9 %all-to-all-done.2 = bf16[128,2,1024]{2,1,0:T(2,128)(2,1)S(1)} async-done(((bf16[128,2,1024]{2,1,0:T(2,128)(2,1)}), bf16[128,2,1024]{2,1,0:T(2,128)(2,1)S(1)}, u32[]{:S(2)}, u32[]{:S(2)}) %all-to-all-start.2) | async-done | bytes 524320 | tf_op jit(solution)/shard_map/all_to_all | solution.py:89
  100.3 4.1 %reshape.663 = bf16[4096,2,2,16]{3,2,1,0:T(2,128)(2,1)} reshape(bf16[128,2,1024]{2,1,0:T(2,128)(2,1)S(1)} %all-to-all-done.2) | data formatting | bytes 1048576
  104.5 8.6 %copy.43 = bf16[16,2,2,128,32]{4,0,2,3,1:T(8,128)(2,1)S(1)} copy(bf16[16,2,2,128,32]{0,1,2,4,3:T(2,128)(2,1)} %bitcast.114) | data formatting | bytes 1048576 | tf_op jit(solution)/shard_map/all_to_all | solution.py:89
  113.0 0.9 bitcast_multiply_fusion
  114.0 1.5 %slice_bitcast_fusion = (f32[16,1,32,512]{3,2,1,0:T(8,128)}, f32[16,1,32,512]{3,2,1,0:T(8,128)}) fusion(f32[16,32,2,512]{3,1,2,0:T(8,128)S(1)} %bitcast_multiply_fusion), kind=kLoop, calls=%fused_computation.6 | loop fusion | bytes 4194304
  (7 shorter events, 0.1 us)
Async XLA Ops:
  0.6 49.8 %copy-start = (bf16[2,2,8,1,4096]{4,2,3,1,0:T(8,128)(2,1)S(1)}, bf16[2,2,8,1,4096]{4,2,3,1,0:T(8,128)(2,1)}, u32[]{:S(2)}) copy-start(bf16[2,2,8,1,4096]{4,2,3,1,0:T(8,128)(2,1)} %param.7) | copy-start | bytes 786436
  36.6 11.1 %all-to-all-start.1 = ((f32[4,1,1024]{2,1,0:T(1,128)}), f32[4,1,1024]{2,1,0:T(1,128)S(1)}, u32[]{:S(2)}, u32[]{:S(2)}) async-start(f32[4,1,1024]{2,1,0:T(1,128)} %reshape.660), calls=%async_computation.1 | async-start | bytes 32768 | tf_op jit(solution)/shard_map/all_to_all | solution.py:77
  57.9 19.3 %copy-start.2 = (s32[3,256]{1,0:T(4,128)S(1)}, s32[3,256]{1,0:T(4,128)}, u32[]{:S(2)}) copy-start(s32[3,256]{1,0:T(4,128)} %param.10) | copy-start | bytes 9220
  57.9 19.3 %copy-start.1 = (s32[3,512]{1,0:T(4,128)S(1)}, s32[3,512]{1,0:T(4,128)}, u32[]{:S(2)}) copy-start(s32[3,512]{1,0:T(4,128)} %param.11) | copy-start | bytes 18436
  70.8 29.5 %all-to-all-start.2 = ((bf16[128,2,1024]{2,1,0:T(2,128)(2,1)}), bf16[128,2,1024]{2,1,0:T(2,128)(2,1)S(1)}, u32[]{:S(2)}, u32[]{:S(2)}) async-start(bf16[128,2,1024]{2,1,0:T(2,128)(2,1)} %reshape.662), calls=%async_computation.2 | async-start | bytes 1048576 | tf_op jit(solution)/shard_map/all_to_all | solution.py:89
